TPU v7x, 128 devices: a whole 4x4x4 slice. The times are simulated.
128 devices in a mesh: row: 4 (over x), col: 32 (over z, y, core).
Axes of the slice: x: 4, y: 4, z: 4, core: 2. Of those that a mesh axis runs over, the one named last changes fastest.
Arguments:
- weights: float32 [6144, 49152], P('row', 'col'), may hold values from -6 to 6
- factor_rows: bfloat16 [8, 128, 49152], P(None, 'row', 'col'), may hold values from -0.25 to 0.25
- panel_inverse: float32 [8, 128, 128], replicated, may hold values from -1 to 2, as said below
- panel_index: int32 [8], replicated, may hold values from 0 to 383, as said below
Outputs:
- pruned: float32 [6144, 49152], P('row', 'col')
Inputs may be any that keep to these rules, and one draw needn't show every extreme that they name: `panel_index`: strictly increasing; the first is always 0 and the last always 49152 // 128 - 1; panel p covers columns p * 128 to p * 128 + 127. Each panel_inverse[k] is upper triangular with a positive diagonal.
All inputs are finite; a program needn't handle non-finite values.
Results may differ from a plain program's by a relative error of at most 0.0064.
Values may be sent and summed in bfloat16 or wider, within the bound.
A program may use at most 128 MiB of HBM per device.

v0:
```python
import jax
import jax.numpy as jnp
from jax import lax
from jax.sharding import PartitionSpec as P


def from_root(value, axis, root):
    mine = lax.axis_index(axis) == root
    return lax.psum(jnp.where(mine, value, jnp.zeros_like(value)), axis)


def local(weights, factor_rows, panel_inverse, panel_index):
    panel_count = panel_inverse.shape[0]
    panel_width = panel_inverse.shape[1]
    col_count = weights.shape[1]
    col_first = lax.axis_index("col") * col_count
    col_ids = col_first + lax.iota(jnp.int32, col_count)
    starts = panel_index * panel_width
    factors = lax.all_gather(factor_rows, "row", axis=1, tiled=True)
    local_starts = jnp.clip(starts - col_first, 0, col_count - panel_width)
    raw_list = []
    cross_list = []
    for number in range(panel_count):
        column_slice = lax.dynamic_slice_in_dim(weights, local_starts[number], panel_width, 1)
        cross_slice = lax.dynamic_slice_in_dim(factors, local_starts[number], panel_width, 2)
        got_columns, got_cross = (
            from_root(column_slice.astype(jnp.bfloat16), "col", starts[number] // col_count).astype(
                column_slice.dtype
            ),
            from_root(cross_slice, "col", starts[number] // col_count),
        )
        raw_list.append(got_columns)
        cross_list.append(got_cross)
    errors = []
    for number in range(panel_count):
        column_slice = raw_list[number]
        for earlier in range(number):
            column_slice = column_slice - jnp.dot(
                errors[earlier], cross_list[number][earlier], preferred_element_type=jnp.float32
            )
        errors.append(
            jnp.dot(
                column_slice,
                panel_inverse[number],
                precision=lax.Precision.HIGHEST,
                preferred_element_type=jnp.float32,
            ).astype(jnp.bfloat16)
        )
    keep_mask = col_ids[None, :] >= (starts + panel_width)[:, None]
    masked = jnp.where(keep_mask[:, None, :], factors, jnp.zeros((), factors.dtype))
    masked = masked.reshape(panel_count * panel_width, col_count)
    current = weights - jnp.dot(
        jnp.concatenate(errors, 1), masked, preferred_element_type=jnp.float32
    )
    pruned_mask = jnp.any((col_ids // panel_width)[:, None] == panel_index[None, :], axis=1)
    return jnp.where(pruned_mask[None, :], 0.0, current)


def solution(mesh):
    placed = (P("row", "col"), P(None, "row", "col"), P(), P())
    return jax.shard_map(
        local, mesh=mesh, in_specs=placed, out_specs=P("row", "col"), check_vma=False
    )
```

profile of v0, /device:TPU:1, one launch (start us, length us, event | category | flops | bytes accessed | tf_op | source)
XLA Modules:
  0.0 212.3 jit_solution(2581814085669990775)
XLA Ops:
  6.5 0.7 all-gather.2.cloned.1.call-update
  8.0 0.7 fusion.28
  38.6 6.9 %fusion.8 = (bf16[1536,128]{1,0:T(8,128)(2,1)}, bf16[1536,128]{1,0:T(8,128)(2,1)}, bf16[1536,128]{1,0:T(8,128)(2,1)}, bf16[1536,128]{1,0:T(8,128)(2,1)}, bf16[15...) fusion(f32[1536,1536]{1,0:T(8,128)} %param.4, ...), kind=kLoop, calls=%fused_computation.54 | loop fusion | flops 1572864 | bytes 6291496 | tf_op jit(solution)/shard_map/jit(_where)/select_n | solution.py:9
  45.5 6.0 %all-gather.2.cloned.1.call-done = bf16[8,128,1536]{2,1,0:T(8,128)(2,1)} async-done(((bf16[8,32,1536]{2,1,0:T(8,128)(2,1)}), bf16[8,128,1536]{2,1,0:T(8,128)(2,1)}) %all-gather.2.cloned.1.call-update) | async-done | bytes 3145744 | tf_op jit(solution)/shard_map/all_gather | solution.py:19
  51.5 4.3 %dynamic-slice_select_fusion = (bf16[8,128,128]{2,1,0:T(8,128)(2,1)}, bf16[8,128,128]{2,1,0:T(8,128)(2,1)}, bf16[8,128,128]{2,1,0:T(8,128)(2,1)}, bf16[8,128,128...) fusion(bf16[8,128,1536]{2,1,0:T(8,128)(2,1)} %all-gather.2.cloned, ...), kind=kLoop, calls=%fused_computation.55 | loop fusion | flops 917504 | bytes 3670051 | tf_op jit(solution)/shard_map/jit(_where)/select_n | solution.py:9
  56.6 1.1 copy-done
  57.7 1.9 broadcast_select_fusion
  59.6 115.5 %all-reduce.3.cloned.1.call-done = (bf16[1536,128]{1,0:T(8,128)(2,1)}, bf16[1536,128]{1,0:T(8,128)(2,1)}, bf16[8,128,128]{2,1,0:T(8,128)(2,1)}, bf16[1536,128]{1...) async-done(((bf16[1536,128]{1,0:T(8,128)(2,1)}, ...) | async-done | bytes 4980752 | tf_op jit(solution)/shard_map/psum | solution.py:9
  175.1 1.6 constant_dynamic-update-slice_fusion.6
  176.7 1.4 convolution_subtract_fusion.6
  178.1 1.3 convolution_subtract_fusion.27
  179.4 0.9 constant_dynamic-update-slice_fusion.5
  180.6 1.0 convolution_subtract_fusion.26
  181.6 1.0 convolution_subtract_fusion.25
  182.7 1.0 convolution_subtract_fusion.24
  183.8 1.0 convolution_subtract_fusion.23
  184.8 0.9 constant_dynamic-update-slice_fusion.4
  186.0 1.1 convolution_subtract_fusion.22
  188.0 0.9 constant_dynamic-update-slice_fusion.3
  190.7 0.9 constant_dynamic-update-slice_fusion.2
  193.7 1.1 constant_dynamic-update-slice_fusion.1
  195.4 0.9 constant_dynamic-update-slice_fusion
  196.6 0.9 fusion
  197.5 8.0 %subtract_select_fusion = f32[1536,1536]{1,0:T(8,128)} fusion(f32[1536,1536]{1,0:T(8,128)S(1)} %bitcast.187, bf16[1536,1024]{0,1:T(8,128)(2,1)S(1)} %fusion, bf16[1024,1536]{1,0:T(8,128)(2,1)S(1)} %bitcast.185, pred[1536]{0:T(1024)(128)(4,1)S(1)} %compare_reduce_fusion), kind=kOutput, calls=%fused_computation | convolution fusion | flops 4836556800 | bytes 25167360 | tf_op jit(solution)/shard_map/dot_general | solution.py:52
  (60 shorter events, 7.8 us)
Async XLA Ops:
  6.5 45.0 %all-gather.2.cloned.1.call-start = ((), (), s32[]{:S(2)}) async-start(), calls=%async_computation | async-start | bytes 3932160 | tf_op jit(solution)/shard_map/all_gather | solution.py:19
  7.3 167.9 %all-reduce.3.cloned.1.call-start = ((), (), s32[]{:S(2)}) async-start(), calls=%async_computation.1 | async-start | bytes 9961472 | tf_op jit(solution)/shard_map/psum | solution.py:9
  55.8 0.7 copy-start.12
  55.8 1.9 copy-start
  59.6 119.8 %copy-start.2 = (f32[8,128,128]{2,1,0:T(8,128)S(1)}, f32[8,128,128]{2,1,0:T(8,128)}, u32[]{:S(2)}) copy-start(f32[8,128,128]{2,1,0:T(8,128)} %param.6) | copy-start | bytes 1572868
  175.1 5.1 %copy-start.8 = (bf16[8,128,128]{2,1,0:T(8,128)(2,1)S(1)}, bf16[8,128,128]{2,1,0:T(8,128)(2,1)}, u32[]{:S(2)}) copy-start(bf16[8,128,128]{2,1,0:T(8,128)(2,1)} %get-tuple-element.19) | copy-start | bytes 786436
  176.7 3.9 %copy-start.7 = (bf16[1536,128]{1,0:T(8,128)(2,1)S(1)}, bf16[1536,128]{1,0:T(8,128)(2,1)}, u32[]{:S(2)}) copy-start(bf16[1536,128]{1,0:T(8,128)(2,1)} %get-tuple-element.8) | copy-start | bytes 1179652
  180.2 2.4 %copy-start.6 = (bf16[1536,128]{1,0:T(8,128)(2,1)S(1)}, bf16[1536,128]{1,0:T(8,128)(2,1)}, u32[]{:S(2)}) copy-start(bf16[1536,128]{1,0:T(8,128)(2,1)} %get-tuple-element.10) | copy-start | bytes 1179652
  184.8 2.2 %copy-start.5 = (bf16[1536,128]{1,0:T(8,128)(2,1)S(1)}, bf16[1536,128]{1,0:T(8,128)(2,1)}, u32[]{:S(2)}) copy-start(bf16[1536,128]{1,0:T(8,128)(2,1)} %get-tuple-element.12) | copy-start | bytes 1179652
  184.8 2.2 %copy-start.11 = (bf16[8,128,128]{2,1,0:T(8,128)(2,1)S(1)}, bf16[8,128,128]{2,1,0:T(8,128)(2,1)}, u32[]{:S(2)}) copy-start(bf16[8,128,128]{2,1,0:T(8,128)(2,1)} %get-tuple-element.13) | copy-start | bytes 786436
  188.0 1.5 copy-start.4
  188.0 1.5 copy-start.10
  189.8 7.7 %slice-start = ((s8[9437184]{0:T(1024)(128)(4,1)}), s8[4194304]{0:T(1024)(128)(4,1)S(1)}, s32[]{:S(2)}) async-start(s8[9437184]{0:T(1024)(128)(4,1)} %bitcast.186), calls=%async_computation.2 | async-start | bytes 8388608
  190.7 1.5 copy-start.3
  190.7 1.5 copy-start.9
  191.9 5.6 %slice-start.1 = ((s8[9437184]{0:T(1024)(128)(4,1)}), s8[4194304]{0:T(1024)(128)(4,1)S(1)}, s32[]{:S(2)}) async-start(s8[9437184]{0:T(1024)(128)(4,1)} %bitcast.186), calls=%async_computation.3 | async-start | bytes 8388608
  193.4 4.0 %slice-start.2 = ((s8[9437184]{0:T(1024)(128)(4,1)}), s8[1048576]{0:T(1024)(128)(4,1)S(1)}, s32[]{:S(2)}) async-start(s8[9437184]{0:T(1024)(128)(4,1)} %bitcast.186), calls=%async_computation.4 | async-start | bytes 2097152
  195.1 2.4 %copy-start.1 = (bf16[8,128,1536]{2,1,0:T(8,128)(2,1)S(1)}, bf16[8,128,1536]{2,1,0:T(8,128)(2,1)}, u32[]{:S(2)}) copy-start(bf16[8,128,1536]{2,1,0:T(8,128)(2,1)} %broadcast_select_fusion) | copy-start | bytes 9437188
Sparse Core Ops, SparseCore 0:
  9.0 42.4 all-gather.1
  57.0 118.1 all-reduce.2
where the time goes:
time: 213 us; the launch traced here: 212 us
  waiting for transfers between devices  122 us (57%)
  between operations  43.8 us (21%)
  matrix products  29.9 us (14%)
  other arithmetic  13.9 us (7%)
  local copies, waits for them, and re-layouts  2.44 us (1%)
    psum x1, waiting for transfers between devices, from_root(): return lax.psum(jnp.where(mine, value, jnp.zeros_like(value)), axis)  116 us
    dot_general x28, matrix products, local(): jnp.dot(errors[earlier], cross_list[number][earlier], preferred_element_t...  14.1 us
    select_n x2, other arithmetic, from_root(): return lax.psum(jnp.where(mine, value, jnp.zeros_like(value)), axis)  11.1 us
    dot_general x1, matrix products, local(): jnp.dot(jnp.concatenate(errors, 1), masked, preferred_element_type=jnp.fl...  8.01 us
    dot_general x8, matrix products, local(): jnp.dot(column_slice, panel_inverse[number], precision=lax.Precision.HIGH...  7.75 us
    all_gather x1, waiting for transfers between devices, local(): factors = lax.all_gather(factor_rows, 'row', axis=1, tiled=True)  5.98 us
  transfers between devices with their start and end apart: 2, of which 2 were waited for; matrix products, arithmetic and copies ran while one was open for 5% of the time, Pallas kernels for 0%

commit v1 on v0

v1 whole, which is shorter than its diff:
```python
import functools

import jax
import jax.numpy as jnp
from jax import lax
from jax.experimental import pallas as pl
from jax.experimental.pallas import tpu as pltpu
from jax.sharding import PartitionSpec as P

MESH = pl.DeviceIdType.MESH
BF16 = jnp.bfloat16
F32 = jnp.float32
PW = 128
NK = 7
KW = NK * PW
NCH = 3
TILES = 24
PAIRS = [(j, k) for k in range(1, NK) for j in range(k)]


def extract_kernel(starts_ref, w_ref, f_ref, raw_ref, cross_ref, wbuf, fbuf, wsem, fsem):
    cols = w_ref.shape[1]

    def copies(k):
        first = pl.multiple_of(starts_ref[k], PW)
        return (
            pltpu.make_async_copy(w_ref.at[:, pl.ds(first, PW)], wbuf.at[k], wsem.at[k]),
            pltpu.make_async_copy(f_ref.at[:, :, pl.ds(first, PW)], fbuf.at[k], fsem.at[k]),
        )

    def mine(k):
        return jnp.logical_and(starts_ref[k] >= 0, starts_ref[k] < cols)

    for k in range(NK):

        @pl.when(mine(k))
        def _():
            for copy in copies(k):
                copy.start()

    cross_ref[...] = jnp.zeros_like(cross_ref)
    for k in range(NK):

        @pl.when(jnp.logical_not(mine(k)))
        def _():
            raw_ref[:, k * PW : (k + 1) * PW] = jnp.zeros((raw_ref.shape[0], PW), BF16)

    for k in range(NK):

        @pl.when(mine(k))
        def _():
            for copy in copies(k):
                copy.wait()
            raw_ref[:, k * PW : (k + 1) * PW] = wbuf[k].astype(BF16)
            for block, (j, kk) in enumerate(PAIRS):
                if kk == k:
                    cross_ref[block] = fbuf[k, j]


def extract(local_starts, weights, factor_rows):
    rows = weights.shape[0]
    depth = factor_rows.shape[1]
    return pl.pallas_call(
        extract_kernel,
        out_shape=(
            jax.ShapeDtypeStruct((rows, KW), BF16),
            jax.ShapeDtypeStruct((TILES, depth, PW), BF16),
        ),
        in_specs=[
            pl.BlockSpec(memory_space=pltpu.SMEM),
            pl.BlockSpec(memory_space=pl.ANY),
            pl.BlockSpec(memory_space=pl.ANY),
        ],
        out_specs=(
            pl.BlockSpec(memory_space=pltpu.VMEM),
            pl.BlockSpec(memory_space=pltpu.VMEM),
        ),
        scratch_shapes=[
            pltpu.VMEM((NK, rows, PW), F32),
            pltpu.VMEM((NK,) + factor_rows.shape[:2] + (PW,), BF16),
            pltpu.SemaphoreType.DMA((NK,)),
            pltpu.SemaphoreType.DMA((NK,)),
        ],
        compiler_params=pltpu.CompilerParams(vmem_limit_bytes=24 << 20),
    )(local_starts, weights, factor_rows)


def exchange_kernel(
    raw_ref, cross_ref, f_ref, pinv_ref, err_ref, fac_ref,
    a_raw, m_raw, r1_raw, acc_raw, r2_raw, s_raw, z1_raw, s2_raw, z2_raw, full_raw,
    a_c, m_c, r1_c, acc_c, r2_c, s_c, z1_c, s2_c, z2_c, x_c, full_c,
    cmat, comp, send_sem, recv_sem, local_sem,
):
    x = lax.axis_index("row")
    col = lax.axis_index("col")
    core = col % 2
    y = (col // 2) % 4
    z = col // 8
    f = y * (1 - core) + z * core
    s = z * (1 - core) + y * core

    def first(v):
        return {"col": (z * (1 - core) + v * core) * 8 + (v * (1 - core) + y * core) * 2 + core}

    def second(v):
        return {"col": (v * (1 - core) + z * core) * 8 + (y * (1 - core) + v * core) * 2 + core}

    def flip1(v):
        return v + 1 - 2 * (v % 2)

    p1, p3 = first(flip1(f)), first(3 - f)
    q1, q3 = second(flip1(s)), second(3 - s)
    x1, x3, x2 = {"row": flip1(x)}, {"row": 3 - x}, {"row": (x + 2) % 4}
    mate = {"col": col + 1 - 2 * core}
    b1, b0 = f // 2, f % 2
    k1, k2 = (b0 + b1) % 2, b1
    l1, l2 = b1, b0

    barrier = pltpu.get_barrier_semaphore()
    for peer in (p1, p3, q1, q3, x1, x2, x3, mate):
        pl.semaphore_signal(barrier, inc=1, device_id=peer, device_id_type=MESH)
    pl.semaphore_wait(barrier, 8)

    count = [0]
    sent = []

    def send(src, dst, peer):
        slot = count[0]
        count[0] += 1
        copy = pltpu.make_async_remote_copy(
            src_ref=src, dst_ref=dst, send_sem=send_sem.at[slot], recv_sem=recv_sem.at[slot],
            device_id=peer, device_id_type=MESH,
        )
        copy.start()
        sent.append(copy)
        return copy

    def arrive(copies):
        for copy in copies:
            copy.wait_recv()

    own = [
        pltpu.make_async_copy(f_ref.at[pl.ds(0, NK), h], fac_ref.at[:, x * 2 + h], local_sem.at[h])
        for h in range(2)
    ]
    fac_waits = []

    def factors_first():
        fac_waits.append(send(f_ref.at[pl.ds(0, NK), 0], fac_ref.at[:, x * 2], x1))
        fac_waits.append(send(f_ref.at[pl.ds(0, NK), 1], fac_ref.at[:, x * 2 + 1], x3))
        for copy in own:
            copy.start()

    def factors_second():
        arrive(fac_waits)
        fac_waits.clear()
        for copy in own:
            copy.wait()
        o1, o3 = flip1(x), 3 - x
        for slot, peer in ((x * 2, x3), (o1 * 2, x3), (x * 2 + 1, x1), (o3 * 2 + 1, x1)):
            fac_waits.append(send(fac_ref.at[:, slot], fac_ref.at[:, slot], peer))

    def reduce_steps(src, a, m, r1, acc, r2, sm, z1, sm2):
        copies = [send(src.at[1 - core], a, mate)]
        yield
        arrive(copies)
        m[...] = src[core] + a[...]
        copies = [send(m.at[0, 1 - k1], r1.at[0], p1), send(m.at[1, 1 - l1], r1.at[1], p3)]
        yield
        arrive(copies)
        acc[0] = m[0, k1] + r1[0]
        acc[1] = m[1, l1] + r1[1]
        copies = [send(acc.at[0, 1 - k2], r2.at[0], p3), send(acc.at[1, 1 - l2], r2.at[1], p1)]
        yield
        arrive(copies)
        sm[0] = acc[0, k2] + r2[0]
        sm[1] = acc[1, l2] + r2[1]
        copies = [send(sm.at[0], z1.at[0], q1), send(sm.at[1], z1.at[1], q3)]
        yield
        arrive(copies)
        sm2[...] = sm[...] + z1[...]

    def gather_steps(full):
        copies = [
            send(full.at[0, k1, k2], full.at[0, k1, k2], p3),
            send(full.at[1, l1, l2], full.at[1, l1, l2], p1),
        ]
        yield
        arrive(copies)
        copies = [send(full.at[0, k1], full.at[0, k1], p1), send(full.at[1, l1], full.at[1, l1], p3)]
        yield
        arrive(copies)

    def cross_steps():
        yield from reduce_steps(cross_ref, a_c, m_c, r1_c, acc_c, r2_c, s_c, z1_c, s2_c)
        copies = [send(s2_c.at[0], z2_c.at[0], q3), send(s2_c.at[1], z2_c.at[1], q1)]
        yield
        arrive(copies)
        x_c[x] = s2_c[...] + z2_c[...]
        copies = [send(x_c.at[x], x_c.at[x], peer) for peer in (x1, x3, x2)]
        yield
        arrive(copies)
        mine = full_c.at[core]
        for t in range(4):
            mine[0, k1, k2, t] = x_c[t, 0]
            mine[1, l1, l2, t] = x_c[t, 1]
        yield from gather_steps(mine)
        copies = [send(mine, mine, mate)]
        yield
        arrive(copies)
        compose()

    def compose():
        for block, (j, k) in enumerate(PAIRS):
            owner, within = block // 12, block % 12
            for half in range(2):
                tile = within * 2 + half
                part, i1, i2, u = tile // 12, tile // 6 % 2, tile // 3 % 2, tile % 3
                for t in range(4):
                    row = j * PW + t * 32 + half * 16
                    cmat[row : row + 16, (k - 1) * PW : k * PW] = full_c[owner, part, i1, i2, t, u]
        comp[...] = jnp.zeros_like(comp)
        for k in range(NK):
            cols = slice(k * PW, (k + 1) * PW)
            comp[cols, cols] = pinv_ref[k].astype(BF16)
            if k:
                top = k * PW
                carried = jnp.dot(
                    comp[:top, :top], cmat[:top, (k - 1) * PW : k * PW], preferred_element_type=F32
                )
                comp[:top, cols] = (
                    -jnp.dot(
                        carried, pinv_ref[k], precision=lax.Precision.HIGHEST, preferred_element_type=F32
                    )
                ).astype(BF16)

    def chunk_steps(c):
        full = full_raw.at[c]
        yield from reduce_steps(
            raw_ref.at[c], a_raw.at[c], m_raw.at[c], r1_raw.at[c], acc_raw.at[c], r2_raw.at[c],
            s_raw.at[c], z1_raw.at[c], s2_raw.at[c],
        )
        s2, z2 = s2_raw.at[c], z2_raw.at[c]
        copies = [send(s2.at[0], z2.at[0], q3), send(s2.at[1], z2.at[1], q1)]
        yield
        arrive(copies)
        full[0, k1, k2] = s2[0] + z2[0]
        full[1, l1, l2] = s2[1] + z2[1]
        yield from gather_steps(full)
        for _ in range(2 - c):
            yield
        rows = err_ref.shape[2]
        panel_cols = full[...].reshape(rows, KW)
        for lo in range(0, KW, 2 * PW):
            hi = min(lo + 2 * PW, KW)
            err_ref[c, core, :, lo:hi] = jnp.dot(
                panel_cols[:, :hi], comp[:hi, lo:hi], preferred_element_type=F32
            ).astype(BF16)
        copies = [send(err_ref.at[c, core], err_ref.at[c, core], mate)]
        yield
        arrive(copies)

    factors_first()
    flows = [(0, cross_steps())] + [(c, chunk_steps(c)) for c in range(NCH)]
    tick = 0
    while flows:
        live = []
        for begin, flow in flows:
            if tick < begin or next(flow, flow) is not flow:
                live.append((begin, flow))
        flows = live
        if tick == 5:
            factors_second()
        tick += 1
    arrive(fac_waits)
    for copy in sent:
        copy.wait_send()


def exchange(raw, cross, factor_rows, panel_inverse):
    cols = factor_rows.shape[2]
    part = raw.shape[0] // (NCH * 16)
    raw = raw.reshape(NCH, 2, 2, 2, 2, part, KW)
    cross = cross.reshape(2, 2, 2, 2, 3, 16, PW)
    factor_rows = factor_rows.reshape(8, 2, 16, cols)
    vm = lambda *shape: pltpu.VMEM(shape, BF16)

    def stages(lead, item):
        return [
            vm(*lead, 2, 2, 2, *item), vm(*lead, 2, 2, 2, *item), vm(*lead, 2, 2, *item),
            vm(*lead, 2, 2, *item), vm(*lead, 2, *item), vm(*lead, 2, *item), vm(*lead, 2, *item),
            vm(*lead, 2, *item), vm(*lead, 2, *item),
        ]

    copies = 2 + 4 + NCH * 14 + 17
    err, fac = pl.pallas_call(
        exchange_kernel,
        out_shape=(
            jax.ShapeDtypeStruct((NCH, 2, 8 * part, KW), BF16),
            jax.ShapeDtypeStruct((NK, 8, 16, cols), BF16),
        ),
        in_specs=[pl.BlockSpec(memory_space=pltpu.VMEM)] * 4,
        out_specs=(pl.BlockSpec(memory_space=pltpu.VMEM),) * 2,
        scratch_shapes=stages((NCH,), (part, KW))
        + [vm(NCH, 2, 2, 2, part, KW)]
        + stages((), (3, 16, PW))
        + [vm(4, 2, 3, 16, PW), vm(2, 2, 2, 2, 4, 3, 16, PW)]
        + [
            vm((NK - 1) * PW, (NK - 1) * PW),
            vm(KW, KW),
            pltpu.SemaphoreType.DMA((copies,)),
            pltpu.SemaphoreType.DMA((copies,)),
            pltpu.SemaphoreType.DMA((2,)),
        ],
        compiler_params=pltpu.CompilerParams(
            collective_id=0, has_side_effects=True, vmem_limit_bytes=48 << 20
        ),
    )(raw, cross, factor_rows, panel_inverse)
    return err.reshape(-1, KW), fac.reshape(KW, cols)


def apply_kernel(starts_ref, w_ref, e_ref, f_ref, o_ref, masked):
    cols = w_ref.shape[1]
    ids = lax.broadcasted_iota(jnp.int32, (1, cols), 1)

    @pl.when(pl.program_id(0) == 0)
    def _():
        for k in range(NK):
            rows = slice(k * PW, (k + 1) * PW)
            keep = ids >= starts_ref[k] + PW
            masked[rows] = jnp.where(keep, f_ref[rows].astype(F32), 0.0).astype(BF16)

    removed = jnp.zeros((1, cols), jnp.bool_)
    for k in range(NK + 1):
        removed = jnp.logical_or(
            removed, jnp.logical_and(ids >= starts_ref[k], ids < starts_ref[k] + PW)
        )
    update = jnp.dot(e_ref[...], masked[...], preferred_element_type=F32)
    o_ref[...] = jnp.where(removed, 0.0, w_ref[...] - update)


def apply(local_starts, weights, err, fac):
    rows, cols = weights.shape
    tile = 256
    return pl.pallas_call(
        apply_kernel,
        out_shape=jax.ShapeDtypeStruct((rows, cols), F32),
        grid=(rows // tile,),
        in_specs=[
            pl.BlockSpec(memory_space=pltpu.SMEM),
            pl.BlockSpec((tile, cols), lambda i: (i, 0)),
            pl.BlockSpec((tile, KW), lambda i: (i, 0)),
            pl.BlockSpec((KW, cols), lambda i: (0, 0)),
        ],
        out_specs=pl.BlockSpec((tile, cols), lambda i: (i, 0)),
        scratch_shapes=[pltpu.VMEM((KW, cols), BF16)],
        compiler_params=pltpu.CompilerParams(vmem_limit_bytes=32 << 20),
    )(local_starts, weights, err, fac)


def local(weights, factor_rows, panel_inverse, panel_index):
    local_starts = panel_index * PW - lax.axis_index("col") * weights.shape[1]
    raw, cross = extract(local_starts, weights, factor_rows)
    err, fac = exchange(raw, cross, factor_rows, panel_inverse)
    return apply(local_starts, weights, err, fac)


def solution(mesh):
    placed = (P("row", "col"), P(None, "row", "col"), P(), P())
    return jax.shard_map(
        local, mesh=mesh, in_specs=placed, out_specs=P("row", "col"), check_vma=False
    )
```

time: 213 us -> 72.2 us (0.34)
  waiting for transfers between devices: 122 us -> 0 us
  Pallas kernels: 0 us -> 61.4 us
  between operations: 43.8 us -> 0.05 us
  matrix products: 29.9 us -> 0 us
  other arithmetic: 13.9 us -> 0.66 us
  local copies, waits for them, and re-layouts: 2.44 us -> 9.91 us
    psum x1 -> x0, waiting for transfers between devices: 116 us -> none  [from_root(): return lax.psum(jnp.where(mine, value, jnp.zeros_like(value)), axis)]
    pallas_call x0 -> x3, Pallas kernels: none -> 61.4 us  [the longest x1 51.8 us: exchange(): pl.pallas_call(exchange_kernel, out_shape=(jax.ShapeDtypeStruct((NCH, 2,...]
    dot_general x37 -> x0, matrix products: 29.9 us -> none  [the longest x28 14.1 us: local(): jnp.dot(errors[earlier], cross_list[number][earlier], preferred_element_t...]
    select_n x4 -> x0, other arithmetic: 13.1 us -> none  [the longest x2 11.1 us: from_root(): return lax.psum(jnp.where(mine, value, jnp.zeros_like(value)), axis)]
    unnamed x32 -> x14, local copies, waits for them, and re-layouts: 1.75 us -> 9.91 us
    all_gather x1 -> x0, waiting for transfers between devices: 5.98 us -> none  [local(): factors = lax.all_gather(factor_rows, 'row', axis=1, tiled=True)]
  transfers between devices with their start and end apart: 2 -> 0, of which waited for: 2 -> 0; matrix products, arithmetic and copies ran while one was open for 5% -> 0% of each run, Pallas kernels for 0% -> 0%
where the time goes in v1:
time: 72.2 us; the launch traced here: 72 us
  Pallas kernels  61.4 us (85%)
  local copies, waits for them, and re-layouts  9.91 us (14%)
    pallas_call x1, Pallas kernels, exchange(): pl.pallas_call(exchange_kernel, out_shape=(jax.ShapeDtypeStruct((NCH, 2,...  51.8 us
    unnamed x14, local copies, waits for them, and re-layouts  9.91 us
    pallas_call x1, Pallas kernels, apply(): pl.pallas_call(apply_kernel, out_shape=jax.ShapeDtypeStruct((rows, cols),...  8.41 us

profile of v1, /device:TPU:1, one launch (start us, length us, event | category | flops | bytes accessed | tf_op | source)
XLA Modules:
  0.0 72.0 jit_solution(13879519224159651100)
XLA Ops:
  0.0 0.7 multiply_subtract_fusion.starts_ref
  0.7 0.0 copy-start
  0.7 3.7 %copy-done = f32[1536,1536]{1,0:T(8,128)S(1)} copy-done((f32[1536,1536]{1,0:T(8,128)S(1)}, f32[1536,1536]{1,0:T(8,128)}, u32[]{:S(2)}) %copy-start) | copy-done | bytes 9437208
  4.3 0.0 copy-start.2
  4.3 1.1 %copy-done.2 = bf16[8,32,1536]{2,1,0:T(8,128)(2,1)S(1)} copy-done((bf16[8,32,1536]{2,1,0:T(8,128)(2,1)S(1)}, bf16[8,32,1536]{2,1,0:T(8,128)(2,1)}, u32[]{:S(2)}) %copy-start.2) | copy-done | bytes 786456
  5.5 0.0 copy-start.3
  5.5 0.0 copy-start.1
  5.5 1.2 %shard_map.46 = (bf16[1536,896]{1,0:T(8,128)(2,1)S(1)}, bf16[24,32,128]{2,1,0:T(8,128)(2,1)S(1)}) custom-call(s32[8]{0:T(128)S(1)} %multiply_subtract_fusion.starts_ref, f32[1536,1536]{1,0:T(8,128)S(1)} %copy-done, bf16[8,32,1536]{2,1,0:T(8,128)(2,1)S(1)} %copy-done.2), custom_call_target="tpu_custom_call" | custom-call | tf_op jit(solution)/shard_map/pallas_call | solution.py:63
  6.7 0.0 copy-start.4
  6.7 1.5 %copy-done.4 = bf16[1536,896]{1,0:T(8,128)(2,1)} copy-done((bf16[1536,896]{1,0:T(8,128)(2,1)}, bf16[1536,896]{1,0:T(8,128)(2,1)S(1)}, u32[]{:S(2)}) %copy-start.4) | copy-done | bytes 2752536
  8.2 0.0 copy-done.3
  8.2 0.0 copy-start.6
  8.2 1.8 %copy-done.6 = f32[8,128,128]{2,1,0:T(8,128)S(1)} copy-done((f32[8,128,128]{2,1,0:T(8,128)S(1)}, f32[8,128,128]{2,1,0:T(8,128)}, u32[]{:S(2)}) %copy-start.6) | copy-done | bytes 524312
  10.0 51.8 %shard_map.47 = (bf16[3,2,256,896]{3,2,1,0:T(8,128)(2,1)S(1)}, bf16[7,8,16,1536]{3,2,1,0:T(8,128)(2,1)}) custom-call(bf16[3,2,2,2,2,32,896]{6,5,4,3,2,1,0:T(8,128)(2,1)} %bitcast.6, bf16[2,2,2,2,3,16,128]{6,5,4,3,2,1,0:T(8,128)(2,1)S(1)} %bitcast.9, bf16[8,2,16,1536]{3,2,1,0:T(8,128)(2,1)S(1)} %bitcast.5, f32[8,128,128]{2,1,0:T(8,128)S(1)} %copy-done.6), custom_call_target="tpu_custom_call" | custom-call | tf_op jit(solution)/shard_map/pallas_call | solution.py:296
  61.8 0.0 copy-done.1
  61.8 0.0 copy-start.5
  61.8 1.8 %copy-done.5 = bf16[7,8,16,1536]{3,2,1,0:T(8,128)(2,1)S(1)} copy-done((bf16[7,8,16,1536]{3,2,1,0:T(8,128)(2,1)S(1)}, bf16[7,8,16,1536]{3,2,1,0:T(8,128)(2,1)}, u32[]{:S(2)}) %copy-start.5) | copy-done | bytes 2752536
  63.6 8.4 %shard_map.48 = f32[1536,1536]{1,0:T(8,128)} custom-call(s32[8]{0:T(128)S(1)} %multiply_subtract_fusion.starts_ref, f32[1536,1536]{1,0:T(8,128)S(1)} %copy-done.1, bf16[1536,896]{1,0:T(8,128)(2,1)S(1)} %bitcast.7, bf16[896,1536]{1,0:T(8,128)(2,1)S(1)} %bitcast.8), custom_call_target="tpu_custom_call" | custom-call | tf_op jit(solution)/shard_map/pallas_call | solution.py:345
Async XLA Ops:
  0.7 3.7 %copy-start = (f32[1536,1536]{1,0:T(8,128)S(1)}, f32[1536,1536]{1,0:T(8,128)}, u32[]{:S(2)}) copy-start(f32[1536,1536]{1,0:T(8,128)} %w_ref.3) | copy-start | bytes 28311556
  4.3 1.1 %copy-start.2 = (bf16[8,32,1536]{2,1,0:T(8,128)(2,1)S(1)}, bf16[8,32,1536]{2,1,0:T(8,128)(2,1)}, u32[]{:S(2)}) copy-start(bf16[8,32,1536]{2,1,0:T(8,128)(2,1)} %f_ref.1) | copy-start | bytes 2359300
  5.5 2.7 %copy-start.3 = (bf16[8,32,1536]{2,1,0:T(8,128)(2,1)S(1)}, bf16[8,32,1536]{2,1,0:T(8,128)(2,1)}, u32[]{:S(2)}) copy-start(bf16[8,32,1536]{2,1,0:T(8,128)(2,1)} %f_ref.1) | copy-start | bytes 2359300
  5.5 56.3 %copy-start.1 = (f32[1536,1536]{1,0:T(8,128)S(1)}, f32[1536,1536]{1,0:T(8,128)}, u32[]{:S(2)}) copy-start(f32[1536,1536]{1,0:T(8,128)} %w_ref.3) | copy-start | bytes 28311556
  6.7 1.5 %copy-start.4 = (bf16[1536,896]{1,0:T(8,128)(2,1)}, bf16[1536,896]{1,0:T(8,128)(2,1)S(1)}, u32[]{:S(2)}) copy-start(bf16[1536,896]{1,0:T(8,128)(2,1)S(1)} %get-tuple-element.9) | copy-start | bytes 8257540
  8.2 1.8 %copy-start.6 = (f32[8,128,128]{2,1,0:T(8,128)S(1)}, f32[8,128,128]{2,1,0:T(8,128)}, u32[]{:S(2)}) copy-start(f32[8,128,128]{2,1,0:T(8,128)} %pinv_ref.1) | copy-start | bytes 1572868
  61.8 1.8 %copy-start.5 = (bf16[7,8,16,1536]{3,2,1,0:T(8,128)(2,1)S(1)}, bf16[7,8,16,1536]{3,2,1,0:T(8,128)(2,1)}, u32[]{:S(2)}) copy-start(bf16[7,8,16,1536]{3,2,1,0:T(8,128)(2,1)} %get-tuple-element.12) | copy-start | bytes 8257540

commit v2 on v1

--- a/solution.py
+++ b/solution.py
@@ -18,18 +18,20 @@
 PAIRS = [(j, k) for k in range(1, NK) for j in range(k)]
 
 
-def extract_kernel(starts_ref, w_ref, f_ref, raw_ref, cross_ref, wbuf, fbuf, wsem, fsem):
+def extract_kernel(index_ref, w_ref, f_ref, raw_ref, cross_ref, wbuf, fbuf, wsem, fsem):
     cols = w_ref.shape[1]
+    here = lax.axis_index("col") * cols
 
     def copies(k):
-        first = pl.multiple_of(starts_ref[k], PW)
+        first = pl.multiple_of(index_ref[k] * PW - here, PW)
         return (
             pltpu.make_async_copy(w_ref.at[:, pl.ds(first, PW)], wbuf.at[k], wsem.at[k]),
             pltpu.make_async_copy(f_ref.at[:, :, pl.ds(first, PW)], fbuf.at[k], fsem.at[k]),
         )
 
     def mine(k):
-        return jnp.logical_and(starts_ref[k] >= 0, starts_ref[k] < cols)
+        first = index_ref[k] * PW - here
+        return jnp.logical_and(first >= 0, first < cols)
 
     for k in range(NK):
 
@@ -57,7 +59,7 @@
                     cross_ref[block] = fbuf[k, j]
 
 
-def extract(local_starts, weights, factor_rows):
+def extract(panel_index, weights, factor_rows):
     rows = weights.shape[0]
     depth = factor_rows.shape[1]
     return pl.pallas_call(
@@ -68,8 +70,8 @@
         ),
         in_specs=[
             pl.BlockSpec(memory_space=pltpu.SMEM),
-            pl.BlockSpec(memory_space=pl.ANY),
-            pl.BlockSpec(memory_space=pl.ANY),
+            pl.BlockSpec(memory_space=pltpu.HBM),
+            pl.BlockSpec(memory_space=pltpu.HBM),
         ],
         out_specs=(
             pl.BlockSpec(memory_space=pltpu.VMEM),
@@ -82,14 +84,14 @@
             pltpu.SemaphoreType.DMA((NK,)),
         ],
         compiler_params=pltpu.CompilerParams(vmem_limit_bytes=24 << 20),
-    )(local_starts, weights, factor_rows)
+    )(panel_index, weights, factor_rows)
 
 
 def exchange_kernel(
-    raw_ref, cross_ref, f_ref, pinv_ref, err_ref, fac_ref,
+    index_ref, raw_ref, cross_ref, f_ref, pinv_hbm, err_ref, masked_ref,
     a_raw, m_raw, r1_raw, acc_raw, r2_raw, s_raw, z1_raw, s2_raw, z2_raw, full_raw,
-    a_c, m_c, r1_c, acc_c, r2_c, s_c, z1_c, s2_c, z2_c, x_c, full_c,
-    cmat, comp, send_sem, recv_sem, local_sem,
+    a_c, m_c, r_c, s_c, z_c, full_c,
+    fac_ref, pinv_ref, cmat, comp, send_sem, recv_sem, local_sem,
 ):
     x = lax.axis_index("row")
     col = lax.axis_index("col")
@@ -112,14 +114,16 @@
     q1, q3 = second(flip1(s)), second(3 - s)
     x1, x3, x2 = {"row": flip1(x)}, {"row": 3 - x}, {"row": (x + 2) % 4}
     mate = {"col": col + 1 - 2 * core}
+    first_others = [first((f + d) % 4) for d in (1, 2, 3)]
+    second_others = [second((s + d) % 4) for d in (1, 2, 3)]
     b1, b0 = f // 2, f % 2
     k1, k2 = (b0 + b1) % 2, b1
     l1, l2 = b1, b0
 
     barrier = pltpu.get_barrier_semaphore()
-    for peer in (p1, p3, q1, q3, x1, x2, x3, mate):
+    for peer in (p1, p3, first_others[1], q1, q3, second_others[1], x1, x2, x3, mate):
         pl.semaphore_signal(barrier, inc=1, device_id=peer, device_id_type=MESH)
-    pl.semaphore_wait(barrier, 8)
+    pl.semaphore_wait(barrier, 10)
 
     count = [0]
     sent = []
@@ -192,20 +196,28 @@
         arrive(copies)
 
     def cross_steps():
-        yield from reduce_steps(cross_ref, a_c, m_c, r1_c, acc_c, r2_c, s_c, z1_c, s2_c)
-        copies = [send(s2_c.at[0], z2_c.at[0], q3), send(s2_c.at[1], z2_c.at[1], q1)]
-        yield
-        arrive(copies)
-        x_c[x] = s2_c[...] + z2_c[...]
-        copies = [send(x_c.at[x], x_c.at[x], peer) for peer in (x1, x3, x2)]
-        yield
-        arrive(copies)
-        mine = full_c.at[core]
-        for t in range(4):
-            mine[0, k1, k2, t] = x_c[t, 0]
-            mine[1, l1, l2, t] = x_c[t, 1]
-        yield from gather_steps(mine)
-        copies = [send(mine, mine, mate)]
+        copies = [send(cross_ref.at[1 - core], a_c, mate)]
+        yield
+        arrive(copies)
+        m_c[...] = cross_ref[core] + a_c[...]
+        copies = [
+            send(m_c.at[(f + d) % 4], r_c.at[d - 1], first_others[d - 1]) for d in (1, 2, 3)
+        ]
+        yield
+        arrive(copies)
+        s_c[...] = m_c[f] + r_c[0] + r_c[1] + r_c[2]
+        copies = [send(s_c, z_c.at[d], second_others[d]) for d in range(3)]
+        yield
+        arrive(copies)
+        mine = full_c.at[core, f]
+        mine[x] = s_c[...] + z_c[0] + z_c[1] + z_c[2]
+        copies = [send(mine.at[x], mine.at[x], peer) for peer in (x1, x3, x2)]
+        yield
+        arrive(copies)
+        copies = [send(mine, mine, peer) for peer in first_others]
+        yield
+        arrive(copies)
+        copies = [send(full_c.at[core], full_c.at[core], mate)]
         yield
         arrive(copies)
         compose()
@@ -215,10 +227,10 @@
             owner, within = block // 12, block % 12
             for half in range(2):
                 tile = within * 2 + half
-                part, i1, i2, u = tile // 12, tile // 6 % 2, tile // 3 % 2, tile % 3
                 for t in range(4):
                     row = j * PW + t * 32 + half * 16
-                    cmat[row : row + 16, (k - 1) * PW : k * PW] = full_c[owner, part, i1, i2, t, u]
+                    cmat[row : row + 16, (k - 1) * PW : k * PW] = full_c[owner, tile // 6, t, tile % 6]
+        pinv_copy.wait()
         comp[...] = jnp.zeros_like(comp)
         for k in range(NK):
             cols = slice(k * PW, (k + 1) * PW)
@@ -247,8 +259,6 @@
         full[0, k1, k2] = s2[0] + z2[0]
         full[1, l1, l2] = s2[1] + z2[1]
         yield from gather_steps(full)
-        for _ in range(2 - c):
-            yield
         rows = err_ref.shape[2]
         panel_cols = full[...].reshape(rows, KW)
         for lo in range(0, KW, 2 * PW):
@@ -260,28 +270,39 @@
         yield
         arrive(copies)
 
+    def mask_factors():
+        arrive(fac_waits)
+        cols = fac_ref.shape[3]
+        ids = lax.broadcasted_iota(jnp.int32, (16, cols), 1) + col * cols
+        for k in range(NK):
+            keep = jnp.where(ids >= index_ref[k] * PW + PW, 1.0, 0.0).astype(BF16)
+            for part in range(8):
+                masked_ref[k, part] = fac_ref[k, part] * keep
+
+    pinv_copy = pltpu.make_async_copy(pinv_hbm, pinv_ref, local_sem.at[2])
+    pinv_copy.start()
     factors_first()
-    flows = [(0, cross_steps())] + [(c, chunk_steps(c)) for c in range(NCH)]
-    tick = 0
-    while flows:
-        live = []
-        for begin, flow in flows:
-            if tick < begin or next(flow, flow) is not flow:
-                live.append((begin, flow))
-        flows = live
-        if tick == 5:
+    cross = cross_steps()
+    chunks = [chunk_steps(c) for c in range(NCH)]
+    for tick in range(7):
+        for flow in [cross] + chunks if tick < 6 else chunks + [cross]:
+            next(flow, None)
+        if tick == 3:
             factors_second()
-        tick += 1
-    arrive(fac_waits)
+    for flow in chunks:
+        next(flow)
+    mask_factors()
+    for flow in chunks:
+        next(flow, None)
     for copy in sent:
         copy.wait_send()
 
 
-def exchange(raw, cross, factor_rows, panel_inverse):
+def exchange(panel_index, raw, cross, factor_rows, panel_inverse):
     cols = factor_rows.shape[2]
     part = raw.shape[0] // (NCH * 16)
     raw = raw.reshape(NCH, 2, 2, 2, 2, part, KW)
-    cross = cross.reshape(2, 2, 2, 2, 3, 16, PW)
+    cross = cross.reshape(2, 4, 6, 16, PW)
     factor_rows = factor_rows.reshape(8, 2, 16, cols)
     vm = lambda *shape: pltpu.VMEM(shape, BF16)
 
@@ -292,56 +313,59 @@
             vm(*lead, 2, *item), vm(*lead, 2, *item),
         ]
 
-    copies = 2 + 4 + NCH * 14 + 17
+    copies = 6 + NCH * 14 + 14
     err, fac = pl.pallas_call(
         exchange_kernel,
         out_shape=(
             jax.ShapeDtypeStruct((NCH, 2, 8 * part, KW), BF16),
             jax.ShapeDtypeStruct((NK, 8, 16, cols), BF16),
         ),
-        in_specs=[pl.BlockSpec(memory_space=pltpu.VMEM)] * 4,
+        in_specs=[
+            pl.BlockSpec(memory_space=pltpu.SMEM),
+            pl.BlockSpec(memory_space=pltpu.VMEM),
+            pl.BlockSpec(memory_space=pltpu.VMEM),
+            pl.BlockSpec(memory_space=pltpu.HBM),
+            pl.BlockSpec(memory_space=pltpu.HBM),
+        ],
         out_specs=(pl.BlockSpec(memory_space=pltpu.VMEM),) * 2,
         scratch_shapes=stages((NCH,), (part, KW))
         + [vm(NCH, 2, 2, 2, part, KW)]
-        + stages((), (3, 16, PW))
-        + [vm(4, 2, 3, 16, PW), vm(2, 2, 2, 2, 4, 3, 16, PW)]
         + [
+            vm(4, 6, 16, PW), vm(4, 6, 16, PW), vm(3, 6, 16, PW), vm(6, 16, PW), vm(3, 6, 16, PW),
+            vm(2, 4, 4, 6, 16, PW),
+            vm(NK, 8, 16, cols),
+            pltpu.VMEM(panel_inverse.shape, F32),
             vm((NK - 1) * PW, (NK - 1) * PW),
             vm(KW, KW),
             pltpu.SemaphoreType.DMA((copies,)),
             pltpu.SemaphoreType.DMA((copies,)),
-            pltpu.SemaphoreType.DMA((2,)),
+            pltpu.SemaphoreType.DMA((3,)),
         ],
         compiler_params=pltpu.CompilerParams(
-            collective_id=0, has_side_effects=True, vmem_limit_bytes=48 << 20
+            collective_id=0, has_side_effects=True, vmem_limit_bytes=28 << 20
         ),
-    )(raw, cross, factor_rows, panel_inverse)
+    )(
+        panel_index, raw, cross,
+        pltpu.with_memory_space_constraint(factor_rows, pltpu.HBM),
+        pltpu.with_memory_space_constraint(panel_inverse, pltpu.HBM),
+    )
     return err.reshape(-1, KW), fac.reshape(KW, cols)
 
 
-def apply_kernel(starts_ref, w_ref, e_ref, f_ref, o_ref, masked):
+def apply_kernel(index_ref, w_ref, e_ref, f_ref, o_ref):
     cols = w_ref.shape[1]
-    ids = lax.broadcasted_iota(jnp.int32, (1, cols), 1)
-
-    @pl.when(pl.program_id(0) == 0)
-    def _():
-        for k in range(NK):
-            rows = slice(k * PW, (k + 1) * PW)
-            keep = ids >= starts_ref[k] + PW
-            masked[rows] = jnp.where(keep, f_ref[rows].astype(F32), 0.0).astype(BF16)
-
+    ids = lax.broadcasted_iota(jnp.int32, (1, cols), 1) + lax.axis_index("col") * cols
     removed = jnp.zeros((1, cols), jnp.bool_)
     for k in range(NK + 1):
-        removed = jnp.logical_or(
-            removed, jnp.logical_and(ids >= starts_ref[k], ids < starts_ref[k] + PW)
-        )
-    update = jnp.dot(e_ref[...], masked[...], preferred_element_type=F32)
+        start = index_ref[k] * PW
+        removed = jnp.logical_or(removed, jnp.logical_and(ids >= start, ids < start + PW))
+    update = jnp.dot(e_ref[...], f_ref[...], preferred_element_type=F32)
     o_ref[...] = jnp.where(removed, 0.0, w_ref[...] - update)
 
 
-def apply(local_starts, weights, err, fac):
+def apply(panel_index, weights, err, fac):
     rows, cols = weights.shape
-    tile = 256
+    tile = 128
     return pl.pallas_call(
         apply_kernel,
         out_shape=jax.ShapeDtypeStruct((rows, cols), F32),
@@ -350,19 +374,18 @@
             pl.BlockSpec(memory_space=pltpu.SMEM),
             pl.BlockSpec((tile, cols), lambda i: (i, 0)),
             pl.BlockSpec((tile, KW), lambda i: (i, 0)),
-            pl.BlockSpec((KW, cols), lambda i: (0, 0)),
+            pl.BlockSpec(memory_space=pltpu.VMEM),
         ],
         out_specs=pl.BlockSpec((tile, cols), lambda i: (i, 0)),
-        scratch_shapes=[pltpu.VMEM((KW, cols), BF16)],
-        compiler_params=pltpu.CompilerParams(vmem_limit_bytes=32 << 20),
-    )(local_starts, weights, err, fac)
+        compiler_params=pltpu.CompilerParams(vmem_limit_bytes=24 << 20),
+    )(panel_index, weights, err, fac)
 
 
 def local(weights, factor_rows, panel_inverse, panel_index):
-    local_starts = panel_index * PW - lax.axis_index("col") * weights.shape[1]
-    raw, cross = extract(local_starts, weights, factor_rows)
-    err, fac = exchange(raw, cross, factor_rows, panel_inverse)
-    return apply(local_starts, weights, err, fac)
+    hbm = lambda v: pltpu.with_memory_space_constraint(v, pltpu.HBM)
+    raw, cross = extract(panel_index, hbm(weights), hbm(factor_rows))
+    err, fac = exchange(panel_index, raw, cross, factor_rows, panel_inverse)
+    return apply(panel_index, weights, err, fac)
 
 
 def solution(mesh):

time: 72.2 us -> 54.1 us (0.75)
  local copies, waits for them, and re-layouts: 9.91 us -> 0.66 us
  Pallas kernels: 61.4 us -> 52.8 us
    pallas_call x1, Pallas kernels: 51.8 us -> 40.7 us  [exchange(): pl.pallas_call(exchange_kernel, out_shape=(jax.ShapeDtypeStruct((NCH, 2,...]
    unnamed x14 -> x6, local copies, waits for them, and re-layouts: 9.91 us -> 0.66 us
    pallas_call x1, Pallas kernels: 8.41 us -> 9.97 us  [apply(): pl.pallas_call(apply_kernel, out_shape=jax.ShapeDtypeStruct((rows, cols),...]
    pallas_call x1, Pallas kernels: 1.19 us -> 2.17 us  [extract(): pl.pallas_call(extract_kernel, out_shape=(jax.ShapeDtypeStruct((rows, KW)...]
where the time goes in v2:
time: 54.1 us; the launch traced here: 53.5 us
  Pallas kernels  52.8 us (98%)
  local copies, waits for them, and re-layouts  0.66 us (1%)
    pallas_call x1, Pallas kernels, exchange(): pl.pallas_call(exchange_kernel, out_shape=(jax.ShapeDtypeStruct((NCH, 2,...  40.7 us
    pallas_call x1, Pallas kernels, apply(): pl.pallas_call(apply_kernel, out_shape=jax.ShapeDtypeStruct((rows, cols),...  9.97 us
    pallas_call x1, Pallas kernels, extract(): pl.pallas_call(extract_kernel, out_shape=(jax.ShapeDtypeStruct((rows, KW)...  2.17 us

profile of v2, /device:TPU:1, one launch (start us, length us, event | category | flops | bytes accessed | tf_op | source)
XLA Modules:
  0.0 53.5 jit_solution(3459584515992767807)
XLA Ops:
  0.0 0.0 copy-start.1
  0.0 0.7 %copy-done.1 = s32[8]{0:T(128)S(1)} copy-done((s32[8]{0:T(128)S(1)}, s32[8]{0:T(128)}, u32[]{:S(2)}) %copy-start.1) | copy-done | bytes 56
  0.7 0.0 copy-start.2
  0.7 0.0 copy-start
  0.7 2.2 %shard_map.46 = (bf16[1536,896]{1,0:T(8,128)(2,1)S(1)}, bf16[24,32,128]{2,1,0:T(8,128)(2,1)S(1)}) custom-call(s32[8]{0:T(128)S(1)} %copy-done.1, f32[1536,1536]{1,0:T(8,128)} %w_ref.3, bf16[8,32,1536]{2,1,0:T(8,128)(2,1)} %f_ref.1), custom_call_target="tpu_custom_call" | custom-call | tf_op jit(solution)/shard_map/pallas_call | solution.py:65
  2.8 0.0 copy-done.2
  2.8 40.7 %shard_map.47 = (bf16[3,2,256,896]{3,2,1,0:T(8,128)(2,1)S(1)}, bf16[7,8,16,1536]{3,2,1,0:T(8,128)(2,1)S(1)}) custom-call(s32[8]{0:T(128)S(1)} %copy-done.2, bf16[3,2,2,2,2,32,896]{6,5,4,3,2,1,0:T(8,128)(2,1)S(1)} %bitcast.5, bf16[2,4,6,16,128]{4,3,2,1,0:T(8,128)(2,1)S(1)} %bitcast.8, bf16[8,2,16,1536]{3,2,1,0:T(8,128)(2,1)} %bitcast.9, f32[8,128,128]{2,1,0:T(8,128)} %pinv_hbm.1), custom_call_target="tpu_custom_call" | custom-call | tf_op jit(solution)/shard_map/pallas_call | solution.py:317
  43.5 0.0 copy-done
  43.5 10.0 %shard_map.48 = f32[1536,1536]{1,0:T(8,128)} custom-call(s32[8]{0:T(128)S(1)} %copy-done.2, f32[1536,1536]{1,0:T(8,128)S(1)} %copy-done, bf16[1536,896]{1,0:T(8,128)(2,1)S(1)} %bitcast.6, bf16[896,1536]{1,0:T(8,128)(2,1)S(1)} %bitcast.7), custom_call_target="tpu_custom_call" | custom-call | tf_op jit(solution)/shard_map/pallas_call | solution.py:369
Async XLA Ops:
  0.0 0.7 %copy-start.1 = (s32[8]{0:T(128)S(1)}, s32[8]{0:T(128)}, u32[]{:S(2)}) copy-start(s32[8]{0:T(128)} %index_ref.5) | copy-start | bytes 100
  0.7 2.2 %copy-start.2 = (s32[8]{0:T(128)S(1)}, s32[8]{0:T(128)}, u32[]{:S(2)}) copy-start(s32[8]{0:T(128)} %index_ref.5) | copy-start | bytes 100
  0.7 42.9 %copy-start = (f32[1536,1536]{1,0:T(8,128)S(1)}, f32[1536,1536]{1,0:T(8,128)}, u32[]{:S(2)}) copy-start(f32[1536,1536]{1,0:T(8,128)} %w_ref.3) | copy-start | bytes 28311556

commit v3 on v2

--- a/solution.py
+++ b/solution.py
@@ -89,7 +89,7 @@
 
 def exchange_kernel(
     index_ref, raw_ref, cross_ref, f_ref, pinv_hbm, err_ref, masked_ref,
-    a_raw, m_raw, r1_raw, acc_raw, r2_raw, s_raw, z1_raw, s2_raw, z2_raw, full_raw,
+    a_raw, m_raw, r1_raw, acc_raw, r4_raw, s_raw, z_raw, full_raw,
     a_c, m_c, r_c, s_c, z_c, full_c,
     fac_ref, pinv_ref, cmat, comp, send_sem, recv_sem, local_sem,
 ):
@@ -101,29 +101,26 @@
     f = y * (1 - core) + z * core
     s = z * (1 - core) + y * core
 
-    def first(v):
-        return {"col": (z * (1 - core) + v * core) * 8 + (v * (1 - core) + y * core) * 2 + core}
-
-    def second(v):
-        return {"col": (v * (1 - core) + z * core) * 8 + (y * (1 - core) + v * core) * 2 + core}
+    def at(ff, ss):
+        yy, zz = ff * (1 - core) + ss * core, ss * (1 - core) + ff * core
+        return {"col": zz * 8 + yy * 2 + core}
 
     def flip1(v):
         return v + 1 - 2 * (v % 2)
 
-    p1, p3 = first(flip1(f)), first(3 - f)
-    q1, q3 = second(flip1(s)), second(3 - s)
+    f1, f3, s1, s3 = flip1(f), 3 - f, flip1(s), 3 - s
     x1, x3, x2 = {"row": flip1(x)}, {"row": 3 - x}, {"row": (x + 2) % 4}
     mate = {"col": col + 1 - 2 * core}
-    first_others = [first((f + d) % 4) for d in (1, 2, 3)]
-    second_others = [second((s + d) % 4) for d in (1, 2, 3)]
-    b1, b0 = f // 2, f % 2
-    k1, k2 = (b0 + b1) % 2, b1
-    l1, l2 = b1, b0
+    first_others = [at((f + d) % 4, s) for d in (1, 2, 3)]
+    second_others = [at(f, (s + d) % 4) for d in (1, 2, 3)]
+    k1, k2, kt = (f % 2 + f // 2) % 2, f // 2, (s % 2 + s // 2) % 2
+    l1, l2, lt = f // 2, f % 2, s // 2
 
     barrier = pltpu.get_barrier_semaphore()
-    for peer in (p1, p3, first_others[1], q1, q3, second_others[1], x1, x2, x3, mate):
+    peers = first_others + second_others + [at(f1, s3), at(f3, s1), x1, x2, x3, mate]
+    for peer in peers:
         pl.semaphore_signal(barrier, inc=1, device_id=peer, device_id_type=MESH)
-    pl.semaphore_wait(barrier, 10)
+    pl.semaphore_wait(barrier, len(peers))
 
     count = [0]
     sent = []
@@ -161,39 +158,11 @@
         for copy in own:
             copy.wait()
         o1, o3 = flip1(x), 3 - x
-        for slot, peer in ((x * 2, x3), (o1 * 2, x3), (x * 2 + 1, x1), (o3 * 2 + 1, x1)):
-            fac_waits.append(send(fac_ref.at[:, slot], fac_ref.at[:, slot], peer))
-
-    def reduce_steps(src, a, m, r1, acc, r2, sm, z1, sm2):
-        copies = [send(src.at[1 - core], a, mate)]
-        yield
-        arrive(copies)
-        m[...] = src[core] + a[...]
-        copies = [send(m.at[0, 1 - k1], r1.at[0], p1), send(m.at[1, 1 - l1], r1.at[1], p3)]
-        yield
-        arrive(copies)
-        acc[0] = m[0, k1] + r1[0]
-        acc[1] = m[1, l1] + r1[1]
-        copies = [send(acc.at[0, 1 - k2], r2.at[0], p3), send(acc.at[1, 1 - l2], r2.at[1], p1)]
-        yield
-        arrive(copies)
-        sm[0] = acc[0, k2] + r2[0]
-        sm[1] = acc[1, l2] + r2[1]
-        copies = [send(sm.at[0], z1.at[0], q1), send(sm.at[1], z1.at[1], q3)]
-        yield
-        arrive(copies)
-        sm2[...] = sm[...] + z1[...]
-
-    def gather_steps(full):
-        copies = [
-            send(full.at[0, k1, k2], full.at[0, k1, k2], p3),
-            send(full.at[1, l1, l2], full.at[1, l1, l2], p1),
-        ]
-        yield
-        arrive(copies)
-        copies = [send(full.at[0, k1], full.at[0, k1], p1), send(full.at[1, l1], full.at[1, l1], p3)]
-        yield
-        arrive(copies)
+        moves = ((x * 2, x3), (x * 2 + 1, x1), (o1 * 2, x3), (o3 * 2 + 1, x1))
+        for k in range(NK):
+            fac_waits.append(
+                [send(fac_ref.at[k, slot], fac_ref.at[k, slot], peer) for slot, peer in moves]
+            )
 
     def cross_steps():
         copies = [send(cross_ref.at[1 - core], a_c, mate)]
@@ -247,18 +216,53 @@
                 ).astype(BF16)
 
     def chunk_steps(c):
-        full = full_raw.at[c]
-        yield from reduce_steps(
-            raw_ref.at[c], a_raw.at[c], m_raw.at[c], r1_raw.at[c], acc_raw.at[c], r2_raw.at[c],
-            s_raw.at[c], z1_raw.at[c], s2_raw.at[c],
-        )
-        s2, z2 = s2_raw.at[c], z2_raw.at[c]
-        copies = [send(s2.at[0], z2.at[0], q3), send(s2.at[1], z2.at[1], q1)]
-        yield
-        arrive(copies)
-        full[0, k1, k2] = s2[0] + z2[0]
-        full[1, l1, l2] = s2[1] + z2[1]
-        yield from gather_steps(full)
+        m, r1, acc, r4 = m_raw.at[c], r1_raw.at[c], acc_raw.at[c], r4_raw.at[c]
+        sm, zr, full = s_raw.at[c], z_raw.at[c], full_raw.at[c]
+        copies = [send(raw_ref.at[c, 1 - core], a_raw.at[c], mate)]
+        yield
+        arrive(copies)
+        m[...] = raw_ref[c, core] + a_raw[c]
+        copies = [
+            send(m.at[0, 1 - k1], r1.at[0], at(f1, s)),
+            send(m.at[1, 1 - l1], r1.at[1], at(f3, s)),
+        ]
+        yield
+        arrive(copies)
+        acc[0] = m[0, k1] + r1[0]
+        acc[1] = m[1, l1] + r1[1]
+        copies = [
+            send(acc.at[0, 1 - k2, 1 - kt], r4.at[0, 2], at(f3, s1)),
+            send(acc.at[1, 1 - l2, 1 - lt], r4.at[1, 2], at(f1, s3)),
+            send(acc.at[0, 1 - k2, kt], r4.at[0, 0], at(f3, s)),
+            send(acc.at[0, k2, 1 - kt], r4.at[0, 1], at(f, s1)),
+            send(acc.at[1, 1 - l2, lt], r4.at[1, 0], at(f1, s)),
+            send(acc.at[1, l2, 1 - lt], r4.at[1, 1], at(f, s3)),
+        ]
+        yield
+        arrive(copies)
+        sm[0] = acc[0, k2, kt] + r4[0, 0] + r4[0, 1] + r4[0, 2]
+        sm[1] = acc[1, l2, lt] + r4[1, 0] + r4[1, 1] + r4[1, 2]
+        copies = [send(sm.at[0], zr.at[0], at(f, s3)), send(sm.at[1], zr.at[1], at(f, s1))]
+        yield
+        arrive(copies)
+        full[0, k1, k2, kt] = sm[0] + zr[0]
+        full[1, l1, l2, lt] = sm[1] + zr[1]
+        piece0, piece1 = full.at[0, k1, k2, kt], full.at[1, l1, l2, lt]
+        copies = [
+            send(piece, piece, peer)
+            for piece, peer in (
+                (piece0, at(f3, s1)), (piece1, at(f1, s3)), (piece0, at(f3, s)),
+                (piece0, at(f, s1)), (piece1, at(f1, s)), (piece1, at(f, s3)),
+            )
+        ]
+        yield
+        arrive(copies)
+        copies = [
+            send(full.at[0, k1], full.at[0, k1], at(f1, s)),
+            send(full.at[1, l1], full.at[1, l1], at(f3, s)),
+        ]
+        yield
+        arrive(copies)
         rows = err_ref.shape[2]
         panel_cols = full[...].reshape(rows, KW)
         for lo in range(0, KW, 2 * PW):
@@ -271,10 +275,10 @@
         arrive(copies)
 
     def mask_factors():
-        arrive(fac_waits)
         cols = fac_ref.shape[3]
         ids = lax.broadcasted_iota(jnp.int32, (16, cols), 1) + col * cols
         for k in range(NK):
+            arrive(fac_waits[k])
             keep = jnp.where(ids >= index_ref[k] * PW + PW, 1.0, 0.0).astype(BF16)
             for part in range(8):
                 masked_ref[k, part] = fac_ref[k, part] * keep
@@ -284,11 +288,12 @@
     factors_first()
     cross = cross_steps()
     chunks = [chunk_steps(c) for c in range(NCH)]
-    for tick in range(7):
-        for flow in [cross] + chunks if tick < 6 else chunks + [cross]:
-            next(flow, None)
+    for tick in range(6):
+        for flow in [cross] + chunks:
+            next(flow)
         if tick == 3:
             factors_second()
+    next(cross, None)
     for flow in chunks:
         next(flow)
     mask_factors()
@@ -300,24 +305,17 @@
 
 def exchange(panel_index, raw, cross, factor_rows, panel_inverse):
     cols = factor_rows.shape[2]
-    part = raw.shape[0] // (NCH * 16)
-    raw = raw.reshape(NCH, 2, 2, 2, 2, part, KW)
+    piece = raw.shape[0] // (NCH * 32)
+    raw = raw.reshape(NCH, 2, 2, 2, 2, 2, piece, KW)
     cross = cross.reshape(2, 4, 6, 16, PW)
     factor_rows = factor_rows.reshape(8, 2, 16, cols)
     vm = lambda *shape: pltpu.VMEM(shape, BF16)
-
-    def stages(lead, item):
-        return [
-            vm(*lead, 2, 2, 2, *item), vm(*lead, 2, 2, 2, *item), vm(*lead, 2, 2, *item),
-            vm(*lead, 2, 2, *item), vm(*lead, 2, *item), vm(*lead, 2, *item), vm(*lead, 2, *item),
-            vm(*lead, 2, *item), vm(*lead, 2, *item),
-        ]
-
-    copies = 6 + NCH * 14 + 14
+    rows = lambda *inner: vm(NCH, 2, *inner, piece, KW)
+    copies = 2 + NK * 4 + NCH * 20 + 14
     err, fac = pl.pallas_call(
         exchange_kernel,
         out_shape=(
-            jax.ShapeDtypeStruct((NCH, 2, 8 * part, KW), BF16),
+            jax.ShapeDtypeStruct((NCH, 2, 16 * piece, KW), BF16),
             jax.ShapeDtypeStruct((NK, 8, 16, cols), BF16),
         ),
         in_specs=[
@@ -328,9 +326,9 @@
             pl.BlockSpec(memory_space=pltpu.HBM),
         ],
         out_specs=(pl.BlockSpec(memory_space=pltpu.VMEM),) * 2,
-        scratch_shapes=stages((NCH,), (part, KW))
-        + [vm(NCH, 2, 2, 2, part, KW)]
-        + [
+        scratch_shapes=[
+            rows(2, 2, 2), rows(2, 2, 2), rows(2, 2), rows(2, 2), rows(3), rows(), rows(),
+            rows(2, 2, 2),
             vm(4, 6, 16, PW), vm(4, 6, 16, PW), vm(3, 6, 16, PW), vm(6, 16, PW), vm(3, 6, 16, PW),
             vm(2, 4, 4, 6, 16, PW),
             vm(NK, 8, 16, cols),
@@ -352,31 +350,38 @@
     return err.reshape(-1, KW), fac.reshape(KW, cols)
 
 
-def apply_kernel(index_ref, w_ref, e_ref, f_ref, o_ref):
-    cols = w_ref.shape[1]
-    ids = lax.broadcasted_iota(jnp.int32, (1, cols), 1) + lax.axis_index("col") * cols
-    removed = jnp.zeros((1, cols), jnp.bool_)
-    for k in range(NK + 1):
-        start = index_ref[k] * PW
-        removed = jnp.logical_or(removed, jnp.logical_and(ids >= start, ids < start + PW))
-    update = jnp.dot(e_ref[...], f_ref[...], preferred_element_type=F32)
-    o_ref[...] = jnp.where(removed, 0.0, w_ref[...] - update)
+def apply_kernel(index_ref, w_ref, e_ref, f_ref, o_hbm, out, sem):
+    rows, cols = w_ref.shape
+    tile = 256
+    here = lax.axis_index("col") * cols
+    copies = []
+    for n, lo in enumerate(range(0, cols, tile)):
+        span = slice(lo, lo + tile)
+        ids = lax.broadcasted_iota(jnp.int32, (1, tile), 1) + (here + lo)
+        removed = jnp.zeros((1, tile), jnp.bool_)
+        for k in range(NK + 1):
+            start = index_ref[k] * PW
+            removed = jnp.logical_or(removed, jnp.logical_and(ids >= start, ids < start + PW))
+        for top in range(0, rows, tile):
+            block = slice(top, top + tile)
+            update = jnp.dot(e_ref[block], f_ref[:, span], preferred_element_type=F32)
+            out[block, span] = jnp.where(removed, 0.0, w_ref[block, span] - update)
+        copy = pltpu.make_async_copy(out.at[:, span], o_hbm.at[:, span], sem.at[n])
+        copy.start()
+        copies.append(copy)
+    for copy in copies:
+        copy.wait()
 
 
 def apply(panel_index, weights, err, fac):
     rows, cols = weights.shape
-    tile = 128
+    whole = pl.BlockSpec(memory_space=pltpu.VMEM)
     return pl.pallas_call(
         apply_kernel,
         out_shape=jax.ShapeDtypeStruct((rows, cols), F32),
-        grid=(rows // tile,),
-        in_specs=[
-            pl.BlockSpec(memory_space=pltpu.SMEM),
-            pl.BlockSpec((tile, cols), lambda i: (i, 0)),
-            pl.BlockSpec((tile, KW), lambda i: (i, 0)),
-            pl.BlockSpec(memory_space=pltpu.VMEM),
-        ],
-        out_specs=pl.BlockSpec((tile, cols), lambda i: (i, 0)),
+        in_specs=[pl.BlockSpec(memory_space=pltpu.SMEM), whole, whole, whole],
+        out_specs=pl.BlockSpec(memory_space=pltpu.HBM),
+        scratch_shapes=[pltpu.VMEM((rows, cols), F32), pltpu.SemaphoreType.DMA((cols // 256,))],
         compiler_params=pltpu.CompilerParams(vmem_limit_bytes=24 << 20),
     )(panel_index, weights, err, fac)
 

time: 54.1 us -> 50.1 us (0.926); the launches traced: 53.5 us -> 50.4 us
  Pallas kernels: 52.8 us -> 49.7 us
    pallas_call x1, Pallas kernels: 9.97 us -> 6.79 us  [apply(): pl.pallas_call(apply_kernel, out_shape=jax.ShapeDtypeStruct((rows, cols),...]
    pallas_call x1, Pallas kernels: 40.7 us -> 41.7 us  [exchange(): pl.pallas_call(exchange_kernel, out_shape=(jax.ShapeDtypeStruct((NCH, 2,...]
    pallas_call x1, Pallas kernels: 2.17 us -> 1.15 us  [extract(): pl.pallas_call(extract_kernel, out_shape=(jax.ShapeDtypeStruct((rows, KW)...]
where the time goes in v3:
time: 50.1 us; the launch traced here: 50.4 us
  Pallas kernels  49.7 us (99%)
  local copies, waits for them, and re-layouts  0.66 us (1%)
    pallas_call x1, Pallas kernels, exchange(): pl.pallas_call(exchange_kernel, out_shape=(jax.ShapeDtypeStruct((NCH, 2,...  41.7 us
    pallas_call x1, Pallas kernels, apply(): pl.pallas_call(apply_kernel, out_shape=jax.ShapeDtypeStruct((rows, cols),...  6.79 us
    pallas_call x1, Pallas kernels, extract(): pl.pallas_call(extract_kernel, out_shape=(jax.ShapeDtypeStruct((rows, KW)...  1.15 us

profile of v3, /device:TPU:1, one launch (start us, length us, event | category | flops | bytes accessed | tf_op | source)
XLA Modules:
  0.0 50.4 jit_solution(2869445251460249020)
XLA Ops:
  0.0 0.0 copy-start.1
  0.0 0.7 %copy-done.1 = s32[8]{0:T(128)S(1)} copy-done((s32[8]{0:T(128)S(1)}, s32[8]{0:T(128)}, u32[]{:S(2)}) %copy-start.1) | copy-done | bytes 56
  0.7 0.0 copy-start.2
  0.7 0.0 copy-start
  0.7 1.2 %shard_map.46 = (bf16[1536,896]{1,0:T(8,128)(2,1)S(1)}, bf16[24,32,128]{2,1,0:T(8,128)(2,1)S(1)}) custom-call(s32[8]{0:T(128)S(1)} %copy-done.1, f32[1536,1536]{1,0:T(8,128)} %w_ref.3, bf16[8,32,1536]{2,1,0:T(8,128)(2,1)} %f_ref.1), custom_call_target="tpu_custom_call" | custom-call | tf_op jit(solution)/shard_map/pallas_call | solution.py:65
  1.8 0.0 copy-done.2
  1.8 41.7 %shard_map.47 = (bf16[3,2,256,896]{3,2,1,0:T(8,128)(2,1)S(1)}, bf16[7,8,16,1536]{3,2,1,0:T(8,128)(2,1)S(1)}) custom-call(s32[8]{0:T(128)S(1)} %copy-done.2, bf16[3,2,2,2,2,2,16,896]{7,6,5,4,3,2,1,0:T(8,128)(2,1)S(1)} %bitcast.5, bf16[2,4,6,16,128]{4,3,2,1,0:T(8,128)(2,1)S(1)} %bitcast.8, bf16[8,2,16,1536]{3,2,1,0:T(8,128)(2,1)} %bitcast.9, ...), custom_call_target="tpu_custom_call" | custom-call | tf_op jit(solution)/shard_map/pallas_call | solution.py:315
  43.6 0.0 copy-done
  43.6 6.8 %shard_map.48 = f32[1536,1536]{1,0:T(8,128)} custom-call(s32[8]{0:T(128)S(1)} %copy-done.2, f32[1536,1536]{1,0:T(8,128)S(1)} %copy-done, bf16[1536,896]{1,0:T(8,128)(2,1)S(1)} %bitcast.6, bf16[896,1536]{1,0:T(8,128)(2,1)S(1)} %bitcast.7), custom_call_target="tpu_custom_call" | custom-call | tf_op jit(solution)/shard_map/pallas_call | solution.py:379
Async XLA Ops:
  0.0 0.7 %copy-start.1 = (s32[8]{0:T(128)S(1)}, s32[8]{0:T(128)}, u32[]{:S(2)}) copy-start(s32[8]{0:T(128)} %index_ref.5) | copy-start | bytes 100
  0.7 1.2 %copy-start.2 = (s32[8]{0:T(128)S(1)}, s32[8]{0:T(128)}, u32[]{:S(2)}) copy-start(s32[8]{0:T(128)} %index_ref.5) | copy-start | bytes 100
  0.7 42.9 %copy-start = (f32[1536,1536]{1,0:T(8,128)S(1)}, f32[1536,1536]{1,0:T(8,128)}, u32[]{:S(2)}) copy-start(f32[1536,1536]{1,0:T(8,128)} %w_ref.3) | copy-start | bytes 28311556

commit v4 on v3

--- a/solution.py
+++ b/solution.py
@@ -87,8 +87,18 @@
     )(panel_index, weights, factor_rows)
 
 
+def removed_columns(index_ref, first, count):
+    ids = lax.broadcasted_iota(jnp.int32, (1, count), 1) + first
+    removed = jnp.zeros((1, count), jnp.bool_)
+    for k in range(NK + 1):
+        start = index_ref[k] * PW
+        removed = jnp.logical_or(removed, jnp.logical_and(ids >= start, ids < start + PW))
+    return removed
+
+
 def exchange_kernel(
-    index_ref, raw_ref, cross_ref, f_ref, pinv_hbm, err_ref, masked_ref,
+    index_ref, raw_ref, cross_ref, w_hbm, f_hbm, pinv_hbm,
+    err_ref, masked_ref, done_ref, w0_ref, w1_ref, w2_ref, f_ref,
     a_raw, m_raw, r1_raw, acc_raw, r4_raw, s_raw, z_raw, full_raw,
     a_c, m_c, r_c, s_c, z_c, full_c,
     fac_ref, pinv_ref, cmat, comp, send_sem, recv_sem, local_sem,
@@ -116,10 +126,23 @@
     k1, k2, kt = (f % 2 + f // 2) % 2, f // 2, (s % 2 + s // 2) % 2
     l1, l2, lt = f // 2, f % 2, s // 2
 
+    w_refs = (w0_ref, w1_ref, w2_ref)
+    band = w0_ref.shape[0]
+    w_copies = [
+        pltpu.make_async_copy(w_hbm.at[c * band : (c + 1) * band], w_refs[c], local_sem.at[c])
+        for c in range(NCH)
+    ]
+    f_copy = pltpu.make_async_copy(f_hbm.at[pl.ds(0, NK)], f_ref, local_sem.at[NCH])
+    f_copy.start()
+    for copy in w_copies:
+        copy.start()
+
     barrier = pltpu.get_barrier_semaphore()
     peers = first_others + second_others + [at(f1, s3), at(f3, s1), x1, x2, x3, mate]
     for peer in peers:
         pl.semaphore_signal(barrier, inc=1, device_id=peer, device_id_type=MESH)
+
+    width = w0_ref.shape[1]
     pl.semaphore_wait(barrier, len(peers))
 
     count = [0]
@@ -141,14 +164,15 @@
             copy.wait_recv()
 
     own = [
-        pltpu.make_async_copy(f_ref.at[pl.ds(0, NK), h], fac_ref.at[:, x * 2 + h], local_sem.at[h])
+        pltpu.make_async_copy(f_ref.at[:, h], fac_ref.at[:, x * 2 + h], local_sem.at[NCH + 1 + h])
         for h in range(2)
     ]
     fac_waits = []
 
     def factors_first():
-        fac_waits.append(send(f_ref.at[pl.ds(0, NK), 0], fac_ref.at[:, x * 2], x1))
-        fac_waits.append(send(f_ref.at[pl.ds(0, NK), 1], fac_ref.at[:, x * 2 + 1], x3))
+        f_copy.wait()
+        fac_waits.append(send(f_ref.at[:, 0], fac_ref.at[:, x * 2], x1))
+        fac_waits.append(send(f_ref.at[:, 1], fac_ref.at[:, x * 2 + 1], x3))
         for copy in own:
             copy.start()
 
@@ -283,40 +307,57 @@
             for part in range(8):
                 masked_ref[k, part] = fac_ref[k, part] * keep
 
-    pinv_copy = pltpu.make_async_copy(pinv_hbm, pinv_ref, local_sem.at[2])
+    pinv_copy = pltpu.make_async_copy(pinv_hbm, pinv_ref, local_sem.at[NCH + 3])
+    def own_block(c):
+        w_copies[c].wait()
+        rows, tile = err_ref.shape[2], 2 * PW
+        for lo in range(0, width, tile):
+            span = slice(lo, lo + tile)
+            factors = masked_ref[:, :, :, span].reshape(KW, tile)
+            update = jnp.dot(err_ref[c, core], factors, preferred_element_type=F32)
+            before = w_refs[c][pl.ds(pl.multiple_of(core * rows, rows), rows), span]
+            removed = removed_columns(index_ref, col * width + lo, tile)
+            done_ref[c, :, span] = jnp.where(removed, 0.0, before - update)
+
     pinv_copy.start()
-    factors_first()
     cross = cross_steps()
     chunks = [chunk_steps(c) for c in range(NCH)]
     for tick in range(6):
         for flow in [cross] + chunks:
             next(flow)
-        if tick == 3:
-            factors_second()
+            if tick == 0 and flow is chunks[0]:
+                factors_first()
+            if tick == 3 and flow is cross:
+                factors_second()
     next(cross, None)
     for flow in chunks:
         next(flow)
     mask_factors()
+    for c in range(NCH):
+        own_block(c)
     for flow in chunks:
         next(flow, None)
     for copy in sent:
         copy.wait_send()
 
 
-def exchange(panel_index, raw, cross, factor_rows, panel_inverse):
+def exchange(panel_index, raw, cross, weights, factor_rows, panel_inverse):
     cols = factor_rows.shape[2]
-    piece = raw.shape[0] // (NCH * 32)
+    piece = weights.shape[0] // (NCH * 32)
+    band = jax.ShapeDtypeStruct((weights.shape[0] // NCH, cols), F32)
     raw = raw.reshape(NCH, 2, 2, 2, 2, 2, piece, KW)
     cross = cross.reshape(2, 4, 6, 16, PW)
     factor_rows = factor_rows.reshape(8, 2, 16, cols)
     vm = lambda *shape: pltpu.VMEM(shape, BF16)
     rows = lambda *inner: vm(NCH, 2, *inner, piece, KW)
     copies = 2 + NK * 4 + NCH * 20 + 14
-    err, fac = pl.pallas_call(
+    err, fac, done, *bands = pl.pallas_call(
         exchange_kernel,
         out_shape=(
             jax.ShapeDtypeStruct((NCH, 2, 16 * piece, KW), BF16),
             jax.ShapeDtypeStruct((NK, 8, 16, cols), BF16),
+            jax.ShapeDtypeStruct((NCH, 16 * piece, cols), F32),
+            band, band, band,
         ),
         in_specs=[
             pl.BlockSpec(memory_space=pltpu.SMEM),
@@ -324,9 +365,11 @@
             pl.BlockSpec(memory_space=pltpu.VMEM),
             pl.BlockSpec(memory_space=pltpu.HBM),
             pl.BlockSpec(memory_space=pltpu.HBM),
+            pl.BlockSpec(memory_space=pltpu.HBM),
         ],
-        out_specs=(pl.BlockSpec(memory_space=pltpu.VMEM),) * 2,
+        out_specs=(pl.BlockSpec(memory_space=pltpu.VMEM),) * 6,
         scratch_shapes=[
+            vm(NK, 2, 16, cols),
             rows(2, 2, 2), rows(2, 2, 2), rows(2, 2), rows(2, 2), rows(3), rows(), rows(),
             rows(2, 2, 2),
             vm(4, 6, 16, PW), vm(4, 6, 16, PW), vm(3, 6, 16, PW), vm(6, 16, PW), vm(3, 6, 16, PW),
@@ -337,60 +380,70 @@
             vm(KW, KW),
             pltpu.SemaphoreType.DMA((copies,)),
             pltpu.SemaphoreType.DMA((copies,)),
-            pltpu.SemaphoreType.DMA((3,)),
+            pltpu.SemaphoreType.DMA((NCH + 4,)),
         ],
         compiler_params=pltpu.CompilerParams(
             collective_id=0, has_side_effects=True, vmem_limit_bytes=28 << 20
         ),
     )(
         panel_index, raw, cross,
+        pltpu.with_memory_space_constraint(weights, pltpu.HBM),
         pltpu.with_memory_space_constraint(factor_rows, pltpu.HBM),
         pltpu.with_memory_space_constraint(panel_inverse, pltpu.HBM),
     )
-    return err.reshape(-1, KW), fac.reshape(KW, cols)
-
-
-def apply_kernel(index_ref, w_ref, e_ref, f_ref, o_hbm, out, sem):
-    rows, cols = w_ref.shape
+    return err, fac.reshape(KW, cols), done, bands
+
+
+def apply_kernel(
+    index_ref, w0_ref, w1_ref, w2_ref, e_ref, f_ref, done_ref, o_hbm, out, sem
+):
+    bands, rows, cols = out.shape
     tile = 256
-    here = lax.axis_index("col") * cols
+    col = lax.axis_index("col")
+    core = col % 2
     copies = []
-    for n, lo in enumerate(range(0, cols, tile)):
-        span = slice(lo, lo + tile)
-        ids = lax.broadcasted_iota(jnp.int32, (1, tile), 1) + (here + lo)
-        removed = jnp.zeros((1, tile), jnp.bool_)
-        for k in range(NK + 1):
-            start = index_ref[k] * PW
-            removed = jnp.logical_or(removed, jnp.logical_and(ids >= start, ids < start + PW))
-        for top in range(0, rows, tile):
-            block = slice(top, top + tile)
-            update = jnp.dot(e_ref[block], f_ref[:, span], preferred_element_type=F32)
-            out[block, span] = jnp.where(removed, 0.0, w_ref[block, span] - update)
-        copy = pltpu.make_async_copy(out.at[:, span], o_hbm.at[:, span], sem.at[n])
+
+    def send(src, band, half, span):
+        top = pl.multiple_of(band * 2 * rows + half * rows, rows)
+        copy = pltpu.make_async_copy(src, o_hbm.at[pl.ds(top, rows), span], sem.at[len(copies)])
         copy.start()
         copies.append(copy)
+
+    for band in range(bands):
+        send(done_ref.at[band], band, core, slice(0, cols))
+    inner = pl.ds(pl.multiple_of((1 - core) * rows, rows), rows)
+    for lo in range(0, cols, tile):
+        span = slice(lo, lo + tile)
+        removed = removed_columns(index_ref, col * cols + lo, tile)
+        for band, w_ref in enumerate((w0_ref, w1_ref, w2_ref)):
+            update = jnp.dot(e_ref[band, 1 - core], f_ref[:, span], preferred_element_type=F32)
+            out[band, :, span] = jnp.where(removed, 0.0, w_ref[inner, span] - update)
+            send(out.at[band, :, span], band, 1 - core, span)
     for copy in copies:
         copy.wait()
 
 
-def apply(panel_index, weights, err, fac):
-    rows, cols = weights.shape
+def apply(panel_index, bands, err, fac, done):
+    cols = fac.shape[1]
     whole = pl.BlockSpec(memory_space=pltpu.VMEM)
     return pl.pallas_call(
         apply_kernel,
-        out_shape=jax.ShapeDtypeStruct((rows, cols), F32),
-        in_specs=[pl.BlockSpec(memory_space=pltpu.SMEM), whole, whole, whole],
+        out_shape=jax.ShapeDtypeStruct((NCH * 2 * done.shape[1], cols), F32),
+        in_specs=[pl.BlockSpec(memory_space=pltpu.SMEM)] + [whole] * 6,
         out_specs=pl.BlockSpec(memory_space=pltpu.HBM),
-        scratch_shapes=[pltpu.VMEM((rows, cols), F32), pltpu.SemaphoreType.DMA((cols // 256,))],
-        compiler_params=pltpu.CompilerParams(vmem_limit_bytes=24 << 20),
-    )(panel_index, weights, err, fac)
+        scratch_shapes=[
+            pltpu.VMEM(done.shape, F32),
+            pltpu.SemaphoreType.DMA((NCH + NCH * (cols // 256),)),
+        ],
+        compiler_params=pltpu.CompilerParams(vmem_limit_bytes=16 << 20),
+    )(panel_index, *bands, err, fac, done)
 
 
 def local(weights, factor_rows, panel_inverse, panel_index):
     hbm = lambda v: pltpu.with_memory_space_constraint(v, pltpu.HBM)
     raw, cross = extract(panel_index, hbm(weights), hbm(factor_rows))
-    err, fac = exchange(panel_index, raw, cross, factor_rows, panel_inverse)
-    return apply(panel_index, weights, err, fac)
+    err, fac, done, bands = exchange(panel_index, raw, cross, weights, factor_rows, panel_inverse)
+    return apply(panel_index, bands, err, fac, done)
 
 
 def solution(mesh):

time: 50.1 us -> 49 us (0.978); the launches traced: 50.4 us -> 48.6 us
  Pallas kernels: 49.7 us -> 47.9 us
    pallas_call x1, Pallas kernels: 6.79 us -> 4.66 us  [apply(): pl.pallas_call(apply_kernel, out_shape=jax.ShapeDtypeStruct((NCH * 2 * do...]
where the time goes in v4:
time: 49 us; the launch traced here: 48.6 us
  Pallas kernels  47.9 us (98%)
  local copies, waits for them, and re-layouts  0.66 us (1%)
    pallas_call x1, Pallas kernels, exchange(): pl.pallas_call(exchange_kernel, out_shape=(jax.ShapeDtypeStruct((NCH, 2,...  42.1 us
    pallas_call x1, Pallas kernels, apply(): pl.pallas_call(apply_kernel, out_shape=jax.ShapeDtypeStruct((NCH * 2 * do...  4.66 us
    pallas_call x1, Pallas kernels, extract(): pl.pallas_call(extract_kernel, out_shape=(jax.ShapeDtypeStruct((rows, KW)...  1.15 us

profile of v4, /device:TPU:1, one launch (start us, length us, event | category | flops | bytes accessed | tf_op | source)
XLA Modules:
  0.0 48.6 jit_solution(15164863906811229943)
XLA Ops:
  0.0 0.0 copy-start
  0.0 0.7 %copy-done = s32[8]{0:T(128)S(1)} copy-done((s32[8]{0:T(128)S(1)}, s32[8]{0:T(128)}, u32[]{:S(2)}) %copy-start) | copy-done | bytes 56
  0.7 0.0 copy-start.1
  0.7 1.2 %shard_map.46 = (bf16[1536,896]{1,0:T(8,128)(2,1)S(1)}, bf16[24,32,128]{2,1,0:T(8,128)(2,1)S(1)}) custom-call(s32[8]{0:T(128)S(1)} %copy-done, f32[1536,1536]{1,0:T(8,128)} %w_hbm.1, bf16[8,32,1536]{2,1,0:T(8,128)(2,1)} %f_ref.1), custom_call_target="tpu_custom_call" | custom-call | tf_op jit(solution)/shard_map/pallas_call | solution.py:65
  1.8 0.0 copy-done.1
  1.8 42.1 %shard_map.47 = (bf16[3,2,256,896]{3,2,1,0:T(8,128)(2,1)S(1)}, bf16[7,8,16,1536]{3,2,1,0:T(8,128)(2,1)S(1)}, f32[3,256,1536]{2,1,0:T(8,128)S(1)}, f32[512,1536]{...) custom-call(s32[8]{0:T(128)S(1)} %copy-done.1, bf16[3,2,2,2,2,2,16,896]{7,6,5,4,3,2,1,0:T(8,128)(2,1)S(1)} %bitcast.4, ...), custom_call_target="tpu_custom_call" | custom-call | tf_op jit(solution)/shard_map/pallas_call | solution.py:354
  43.9 4.7 %shard_map.48 = f32[1536,1536]{1,0:T(8,128)} custom-call(s32[8]{0:T(128)S(1)} %copy-done.1, f32[512,1536]{1,0:T(8,128)S(1)} %get-tuple-element.15.w0_ref, f32[512,1536]{1,0:T(8,128)S(1)} %get-tuple-element.16.w1_ref, f32[512,1536]{1,0:T(8,128)S(1)} %get-tuple-element.17.w2_ref, bf16[3,2,256,896]{3,2,1,0:T(8,128)(2,1)S(1)} %get-tuple-element.18.e_ref, ...), custom_call_target="tpu_custom_call" | custom-call | tf_op jit(solution)/shard_map/pallas_call | solution.py:429
Async XLA Ops:
  0.0 0.7 %copy-start = (s32[8]{0:T(128)S(1)}, s32[8]{0:T(128)}, u32[]{:S(2)}) copy-start(s32[8]{0:T(128)} %index_ref.5) | copy-start | bytes 100
  0.7 1.2 %copy-start.1 = (s32[8]{0:T(128)S(1)}, s32[8]{0:T(128)}, u32[]{:S(2)}) copy-start(s32[8]{0:T(128)} %index_ref.5) | copy-start | bytes 100

commit v5 on v4

--- a/solution.py
+++ b/solution.py
@@ -18,7 +18,9 @@
 PAIRS = [(j, k) for k in range(1, NK) for j in range(k)]
 
 
-def extract_kernel(index_ref, w_ref, f_ref, raw_ref, cross_ref, wbuf, fbuf, wsem, fsem):
+def extract_kernel(
+    index_hbm, w_ref, f_ref, raw_ref, cross_ref, index_ref, wbuf, fbuf, isem, wsem, fsem
+):
     cols = w_ref.shape[1]
     here = lax.axis_index("col") * cols
 
@@ -33,19 +35,17 @@
         first = index_ref[k] * PW - here
         return jnp.logical_and(first >= 0, first < cols)
 
+    index_copy = pltpu.make_async_copy(index_hbm, index_ref, isem)
+    index_copy.start()
+    cross_ref[...] = jnp.zeros_like(cross_ref)
+    raw_ref[...] = jnp.zeros_like(raw_ref)
+    index_copy.wait()
     for k in range(NK):
 
         @pl.when(mine(k))
         def _():
             for copy in copies(k):
                 copy.start()
-
-    cross_ref[...] = jnp.zeros_like(cross_ref)
-    for k in range(NK):
-
-        @pl.when(jnp.logical_not(mine(k)))
-        def _():
-            raw_ref[:, k * PW : (k + 1) * PW] = jnp.zeros((raw_ref.shape[0], PW), BF16)
 
     for k in range(NK):
 
@@ -69,7 +69,7 @@
             jax.ShapeDtypeStruct((TILES, depth, PW), BF16),
         ),
         in_specs=[
-            pl.BlockSpec(memory_space=pltpu.SMEM),
+            pl.BlockSpec(memory_space=pltpu.HBM),
             pl.BlockSpec(memory_space=pltpu.HBM),
             pl.BlockSpec(memory_space=pltpu.HBM),
         ],
@@ -78,8 +78,10 @@
             pl.BlockSpec(memory_space=pltpu.VMEM),
         ),
         scratch_shapes=[
+            pltpu.SMEM(panel_index.shape, jnp.int32),
             pltpu.VMEM((NK, rows, PW), F32),
             pltpu.VMEM((NK,) + factor_rows.shape[:2] + (PW,), BF16),
+            pltpu.SemaphoreType.DMA,
             pltpu.SemaphoreType.DMA((NK,)),
             pltpu.SemaphoreType.DMA((NK,)),
         ],
@@ -441,7 +443,7 @@
 
 def local(weights, factor_rows, panel_inverse, panel_index):
     hbm = lambda v: pltpu.with_memory_space_constraint(v, pltpu.HBM)
-    raw, cross = extract(panel_index, hbm(weights), hbm(factor_rows))
+    raw, cross = extract(hbm(panel_index), hbm(weights), hbm(factor_rows))
     err, fac, done, bands = exchange(panel_index, raw, cross, weights, factor_rows, panel_inverse)
     return apply(panel_index, bands, err, fac, done)
 

time: 49 us -> 48.3 us (0.986)
  local copies, waits for them, and re-layouts: 0.66 us -> 0.01 us
    unnamed x4 -> x2, local copies, waits for them, and re-layouts: 0.66 us -> 0.01 us
where the time goes in v5:
time: 48.3 us; the launch traced here: 48.2 us
  Pallas kernels  48.1 us (100%)
    pallas_call x1, Pallas kernels, exchange(): pl.pallas_call(exchange_kernel, out_shape=(jax.ShapeDtypeStruct((NCH, 2,...  42.4 us
    pallas_call x1, Pallas kernels, apply(): pl.pallas_call(apply_kernel, out_shape=jax.ShapeDtypeStruct((NCH * 2 * do...  4.66 us
    pallas_call x1, Pallas kernels, extract(): pl.pallas_call(extract_kernel, out_shape=(jax.ShapeDtypeStruct((rows, KW)...  1.03 us

profile of v5, /device:TPU:1, one launch (start us, length us, event | category | flops | bytes accessed | tf_op | source)
XLA Modules:
  0.0 48.2 jit_solution(9718788518318262183)
XLA Ops:
  0.0 0.0 copy-start
  0.0 1.0 %shard_map.46 = (bf16[1536,896]{1,0:T(8,128)(2,1)S(1)}, bf16[24,32,128]{2,1,0:T(8,128)(2,1)S(1)}) custom-call(s32[8]{0:T(128)} %index_ref.3, f32[1536,1536]{1,0:T(8,128)} %w_hbm.1, bf16[8,32,1536]{2,1,0:T(8,128)(2,1)} %f_ref.1), custom_call_target="tpu_custom_call" | custom-call | tf_op jit(solution)/shard_map/pallas_call | solution.py:65
  1.0 0.0 copy-done
  1.0 42.4 %shard_map.47 = (bf16[3,2,256,896]{3,2,1,0:T(8,128)(2,1)S(1)}, bf16[7,8,16,1536]{3,2,1,0:T(8,128)(2,1)S(1)}, f32[3,256,1536]{2,1,0:T(8,128)S(1)}, f32[512,1536]{...) custom-call(s32[8]{0:T(128)S(1)} %copy-done, bf16[3,2,2,2,2,2,16,896]{7,6,5,4,3,2,1,0:T(8,128)(2,1)S(1)} %bitcast.4, ...), custom_call_target="tpu_custom_call" | custom-call | tf_op jit(solution)/shard_map/pallas_call | solution.py:356
  43.5 4.7 %shard_map.48 = f32[1536,1536]{1,0:T(8,128)} custom-call(s32[8]{0:T(128)S(1)} %copy-done, f32[512,1536]{1,0:T(8,128)S(1)} %get-tuple-element.15.w0_ref, f32[512,1536]{1,0:T(8,128)S(1)} %get-tuple-element.16.w1_ref, f32[512,1536]{1,0:T(8,128)S(1)} %get-tuple-element.17.w2_ref, bf16[3,2,256,896]{3,2,1,0:T(8,128)(2,1)S(1)} %get-tuple-element.18.e_ref, ...), custom_call_target="tpu_custom_call" | custom-call | tf_op jit(solution)/shard_map/pallas_call | solution.py:431
Async XLA Ops:
  0.0 1.0 %copy-start = (s32[8]{0:T(128)S(1)}, s32[8]{0:T(128)}, u32[]{:S(2)}) copy-start(s32[8]{0:T(128)} %index_ref.3) | copy-start | bytes 100
